TPU v7x, 32 devices: a whole 2x2x4 slice. The times are simulated.
32 devices in a mesh: outer: 4 (over y, x), inner: 8 (over z, core).
Axes of the slice: x: 2, y: 2, z: 4, core: 2. Of those that a mesh axis runs over, the one named last changes fastest.
Arguments:
- queries: bfloat16 [8192, 16, 128], P(('outer', 'inner')), may hold values from -6 to 6
- key_rows: bfloat16 [8192, 16, 128], P(('outer', 'inner')), may hold values from -6 to 6
- value_rows: bfloat16 [8192, 16, 128], P(('outer', 'inner')), may hold values from -6 to 6
- key_scale: bfloat16 [8192, 16], P(('outer', 'inner')), may hold values from 0.5 to 2
- value_scale: bfloat16 [8192, 16], P(('outer', 'inner')), may hold values from 0.5 to 2
- cluster_label: int32 [16, 8192, 1], P(None, ('outer', 'inner')), may hold values from 0 to 127; in each aligned block of 256 rows (0 to 255, 256 to 511, ..., all dimensions but the last counted through in order) at most 4 rows name the same one
Outputs:
- attended: bfloat16 [8192, 16, 128], P(('outer', 'inner'))
Inputs may be any that keep to these rules, and one draw needn't show every extreme that they name: `cluster_label`: among the 256 rows of one device for one head, no label occurs more than 4 times, and some label occurs exactly 4 times.
All inputs are finite; a program needn't handle non-finite values.
Results may differ from a plain program's by a relative error of at most 0.0033.
Values may be sent and summed in bfloat16 or wider, within the bound.
A program may use at most 64 MiB of HBM per device.

v0:
```python
import jax
import jax.numpy as jnp
from jax import lax
from jax.experimental import pallas as pl
from jax.experimental.pallas import tpu as pltpu
from jax.sharding import PartitionSpec as P

COARSE = 16
FINE = 8


def attend(query_block, key_block, value_block, key_factor, value_factor, position):
    factor = query_block.shape[-1] ** (-0.5)
    scores = jnp.dot(query_block, key_block.T, preferred_element_type=jnp.float32)
    scores = scores * (key_factor.astype(jnp.float32) * factor)[None, :]
    visible = (position[None, :] >= 0) & (position[None, :] <= position[:, None])
    highest = jnp.max(jnp.where(visible, scores, jnp.float32(-1e30)), axis=1, keepdims=True)
    unnormed = jnp.where(visible, jnp.exp(scores - highest), jnp.float32(0.0))
    denominator = jnp.sum(unnormed, axis=1)
    weights = (unnormed * value_factor.astype(jnp.float32)[None, :]).astype(jnp.bfloat16)
    numerator = jnp.dot(weights, value_block, preferred_element_type=jnp.float32)
    safe = jnp.where(denominator > 0, denominator, jnp.float32(1.0))
    return (numerator / safe[:, None]).astype(jnp.bfloat16)


def attend_items(query_part, key_part, value_part, key_factor, value_factor, position):
    leading = query_part.shape[:3]
    slots = query_part.shape[3]
    width = query_part.shape[4]
    total = leading[0] * leading[1] * leading[2]

    def single(inputs):
        return attend(*inputs)

    results = lax.map(
        single,
        (
            query_part.reshape(total, slots, width),
            key_part.reshape(total, slots, width),
            value_part.reshape(total, slots, width),
            key_factor.reshape(total, slots),
            value_factor.reshape(total, slots),
            position.reshape(total, slots),
        ),
    )
    return results.reshape(leading + (slots, width))


def shards(queries, key_rows, value_rows, key_scale, value_scale, cluster_label):
    outer_count = lax.axis_size("outer")
    inner_count = lax.axis_size("inner")
    tok_rows, heads, width = queries.shape
    cluster_count = COARSE * FINE
    capacity = max(2, 2 * tok_rows // cluster_count)
    labels = cluster_label[:, :, 0].T
    member = (
        labels[:, :, None] == jnp.arange(cluster_count, dtype=jnp.int32)[None, None, :]
    ).astype(jnp.int32)
    rank = jnp.sum(jnp.cumsum(member, axis=0) * member, axis=2) - 1
    slot = (labels * heads + jnp.arange(heads, dtype=jnp.int32)[None, :]) * capacity + rank
    flat = slot.reshape(-1)
    total = cluster_count * heads * capacity
    item_count = cluster_count * heads // (outer_count * inner_count)
    layout = (outer_count, inner_count, item_count, capacity)
    source = (
        jnp.full((total,), -1, jnp.int32)
        .at[flat]
        .set(jnp.arange(tok_rows * heads, dtype=jnp.int32))
    )
    filled_slot = source >= 0
    source_row = jnp.maximum(source, 0)

    def place(array):
        rows = array.reshape((tok_rows * heads,) + array.shape[2:])
        picked = rows[source_row]
        mask = filled_slot.reshape((total,) + (1,) * (picked.ndim - 1))
        kept = jnp.where(mask, picked, jnp.zeros((), array.dtype))
        return kept.reshape(layout + array.shape[2:])

    device = lax.axis_index("outer") * inner_count + lax.axis_index("inner")
    position_rows = jnp.where(filled_slot, device * tok_rows + source_row // heads, -1).reshape(
        layout
    )
    outgoing = (
        place(queries),
        place(key_rows),
        place(value_rows),
        place(key_scale),
        place(value_scale),
        position_rows,
    )
    arrived = (
        lax.all_to_all(
            lax.all_to_all(outgoing[0], "outer", split_axis=0, concat_axis=3, tiled=True),
            "inner",
            split_axis=1,
            concat_axis=3,
            tiled=True,
        ),
        lax.all_to_all(
            lax.all_to_all(outgoing[1], "outer", split_axis=0, concat_axis=3, tiled=True),
            "inner",
            split_axis=1,
            concat_axis=3,
            tiled=True,
        ),
        lax.all_to_all(
            lax.all_to_all(outgoing[2], "outer", split_axis=0, concat_axis=3, tiled=True),
            "inner",
            split_axis=1,
            concat_axis=3,
            tiled=True,
        ),
        lax.all_to_all(
            lax.all_to_all(outgoing[3], "outer", split_axis=0, concat_axis=3, tiled=True),
            "inner",
            split_axis=1,
            concat_axis=3,
            tiled=True,
        ),
        lax.all_to_all(
            lax.all_to_all(outgoing[4], "outer", split_axis=0, concat_axis=3, tiled=True),
            "inner",
            split_axis=1,
            concat_axis=3,
            tiled=True,
        ),
        lax.all_to_all(
            lax.all_to_all(outgoing[5], "outer", split_axis=0, concat_axis=3, tiled=True),
            "inner",
            split_axis=1,
            concat_axis=3,
            tiled=True,
        ),
    )
    answered = attend_items(*arrived)
    returned = lax.all_to_all(
        lax.all_to_all(answered, "inner", split_axis=3, concat_axis=1, tiled=True),
        "outer",
        split_axis=3,
        concat_axis=0,
        tiled=True,
    )
    rows_back = returned.reshape(total, width)
    return rows_back[flat].reshape(tok_rows, heads, width)

AUX = 8


def exchange_kernel(
    chips, half, tok, slots, x_ref, o_ref, recv, ans, kp, vp, xp, qp, op, kb, vb, scales, vis_ref,
    send_sem, recv_sem, fsend, frecv, qsend, qrecv, bsend, brecv,
):
    f32, bf16 = jnp.float32, jnp.bfloat16
    width = x_ref.shape[2]
    inner = lax.axis_index("inner")
    chip = lax.axis_index("outer") * half + inner // 2
    core = inner % 2
    partner = {"outer": lax.axis_index("outer"), "inner": inner + 1 - 2 * core}
    first = x_ref.shape[1] - tok
    first_rows, query_rows = pl.ds(0, first), pl.ds(first, tok)

    def at(other):
        return {"outer": other // half, "inner": (other % half) * 2 + core}

    def copy(src, dst, s1, s2, where):
        return pltpu.make_async_remote_copy(
            src_ref=src, dst_ref=dst, send_sem=s1, recv_sem=s2,
            device_id=where, device_id_type=pl.DeviceIdType.MESH,
        )

    barrier = pltpu.get_barrier_semaphore()

    @pl.loop(1, chips)
    def _(d):
        pl.semaphore_signal(
            barrier, inc=1, device_id=at((chip + d) % chips),
            device_id_type=pl.DeviceIdType.MESH,
        )

    pl.semaphore_signal(
        barrier, inc=1, device_id=partner, device_id_type=pl.DeviceIdType.MESH
    )
    pl.semaphore_wait(barrier, chips)

    def outgoing(d):
        other = chip ^ d
        return copy(
            x_ref.at[other, first_rows], recv.at[2 * chip + core, first_rows],
            send_sem.at[d], recv_sem.at[d], at(other),
        )

    def outgoing_query(d):
        other = chip ^ d
        return copy(
            x_ref.at[other, query_rows], recv.at[2 * chip + core, query_rows],
            qsend.at[d], qrecv.at[d], at(other),
        )

    @pl.loop(1, chips)
    def _(d):
        outgoing(d).start()

    @pl.loop(1, chips)
    def _(d):
        outgoing_query(d).start()

    def own_forward():
        return copy(
            x_ref.at[chip, first_rows], recv.at[2 * chip + core, first_rows],
            fsend.at[0], frecv.at[0], partner,
        )

    def forward(d):
        row = 2 * (chip ^ d) + core
        return copy(
            recv.at[row, first_rows], recv.at[row, first_rows], fsend.at[d], frecv.at[d], partner
        )

    own_forward().start()
    recv[2 * chip + core] = x_ref[chip]

    lane = lax.broadcasted_iota(jnp.int32, (tok, width), 1)
    low = (lane < width // 2).astype(f32).astype(bf16)
    high = (lane >= width // 2).astype(f32).astype(bf16)
    key_at = lax.broadcasted_iota(jnp.int32, vis_ref.shape, 1)
    query_at = lax.broadcasted_iota(jnp.int32, vis_ref.shape, 0)
    key_order = (key_at // 8) * 4 + key_at % 4
    query_order = (2 * (query_at // 8) + core) * 4 + query_at % 4
    same = (key_at // 4) % 2 == (query_at // 4) % 2
    vis_ref[...] = jnp.where(same & (key_order <= query_order), f32(1.0), f32(0.0))
    halves = tok // width

    def aux_of(row):
        block = recv[row, pl.ds(2 * tok, AUX * halves)].astype(f32)
        return jnp.concatenate(
            [block[AUX * i : AUX * (i + 1)] for i in range(halves)], axis=1
        )

    def hits(aux):
        slot = (aux[2:3] + aux[3:4]).astype(jnp.int32)
        return lax.broadcasted_iota(jnp.int32, (slots, tok), 0) == slot

    def one_hot(hit):
        return jnp.where(hit, f32(1.0), f32(0.0)).astype(bf16)

    def place(row):
        aux = aux_of(row)
        hit = hits(aux)
        one = one_hot(hit)
        by_key = jnp.where(hit, aux[0:1], f32(0.0)).astype(bf16)
        by_value = jnp.where(hit, aux[1:2], f32(0.0)).astype(bf16)
        kp[row] = jnp.dot(one, recv[row, pl.ds(0, tok)], preferred_element_type=f32)
        vp[row] = jnp.dot(one, recv[row, pl.ds(tok, tok)], preferred_element_type=f32)
        xp[row] = jnp.dot(by_key, low, preferred_element_type=f32) + jnp.dot(
            by_value, high, preferred_element_type=f32
        )

    def place_query(other):
        row = 2 * other + core
        qp[other] = jnp.dot(
            one_hot(hits(aux_of(row))), recv[row, query_rows], preferred_element_type=f32
        )

    place(2 * chip + core)

    @pl.loop(1, chips)
    def _(d):
        outgoing(d).wait_recv()
        forward(d).start()
        place(2 * (chip ^ d) + core)

        @pl.when(d == 1)
        def _():
            own_forward().wait_recv()

        @pl.when(d > 1)
        def _():
            forward(d - 1).wait_recv()

        place(2 * (chip ^ (d - 1)) + 1 - core)

    forward(chips - 1).wait_recv()
    place(2 * (chip ^ (chips - 1)) + 1 - core)

    sel_lane = lax.broadcasted_iota(jnp.int32, (16, width), 1)
    sel_row = lax.broadcasted_iota(jnp.int32, (16, width), 0)
    select = (sel_lane == jnp.where(sel_row < 8, 0, width // 2)).astype(f32).astype(bf16)
    factor = width ** (-0.5)
    keys_here = vis_ref.shape[1]
    chunk_rows = CHUNK * 8
    nt = (((1,), (1,)), ((), ()))

    def rows_of(t):
        return pl.ds(pl.multiple_of(t * 8, 8), 8)

    @pl.loop(0, slots // 8 // UNROLL)
    def _(at_group):
        for u in range(UNROLL):
            t = at_group * UNROLL + u
            rows = rows_of(t)
            kb[t] = kp[:, rows, :].reshape(keys_here, width).astype(bf16)
            vb[t] = vp[:, rows, :].reshape(keys_here, width).astype(bf16)
            extra = xp[:, rows, :].reshape(keys_here, width).astype(bf16)
            scales[t] = lax.dot_general(select, extra, nt, preferred_element_type=f32)

    def attend_groups(base, groups):
        here = pl.ds(base, CHUNK)
        allowed = vis_ref[pl.ds(pl.multiple_of(base * 8, chunk_rows), chunk_rows), :]
        scale = [scales[t] for t in groups]
        query = [qp[here, rows_of(t), :].reshape(chunk_rows, width).astype(bf16) for t in groups]
        scores = [
            lax.dot_general(q, kb[t], nt, preferred_element_type=f32)
            for q, t in zip(query, groups)
        ]
        visible = [allowed * c[0:1] > 0 for c in scale]
        scores = [
            jnp.where(ok, s * (c[0:1] * factor), f32(-1e30))
            for ok, s, c in zip(visible, scores, scale)
        ]
        highest = [jnp.max(s, axis=1, keepdims=True) for s in scores]
        unnormed = [
            jnp.where(ok, jnp.exp(s - m), f32(0.0))
            for ok, s, m in zip(visible, scores, highest)
        ]
        weights = [(e * c[8:9]).astype(bf16) for e, c in zip(unnormed, scale)]
        numerator = [
            jnp.dot(w, vb[t], preferred_element_type=f32) for w, t in zip(weights, groups)
        ]
        denominator = [jnp.sum(e, axis=1, keepdims=True) for e in unnormed]
        safe = [jnp.where(n > 0, n, f32(1.0)) for n in denominator]
        result = [(n / d).astype(bf16).astype(f32) for n, d in zip(numerator, safe)]
        for r, t in zip(result, groups):
            op[here, rows_of(t), :] = r.reshape(CHUNK, 8, width)

    eye = (
        lax.broadcasted_iota(jnp.int32, (tok, tok), 0)
        == lax.broadcasted_iota(jnp.int32, (tok, tok), 1)
    ).astype(f32).astype(bf16)

    def answer(other):
        columns = lax.dot_general(
            eye,
            aux_of(2 * other + core).astype(bf16),
            (((1,), (1,)), ((), ())),
            preferred_element_type=f32,
        )
        slot = (columns[:, 2:3] + columns[:, 3:4]).astype(jnp.int32)
        hit = lax.broadcasted_iota(jnp.int32, (tok, slots), 1) == slot
        one = jnp.where(hit, f32(1.0), f32(0.0)).astype(bf16)
        return jnp.dot(one, op[other].astype(bf16), preferred_element_type=f32).astype(bf16)

    def reply(d):
        other = chip ^ d
        return copy(ans.at[other], o_ref.at[chip], bsend.at[d], brecv.at[d], at(other))

    def finish(first_d, last_d):
        @pl.loop(first_d, last_d)
        def _(d):
            other = chip ^ d
            ans[other] = answer(other)

            @pl.when(d > first_d)
            def _():
                reply(d - 1).start()

        reply(last_d - 1).start()

    place_query(chip)
    for part in range(chips // CHUNK):
        first_d = part * CHUNK

        @pl.loop(max(first_d, 1), first_d + CHUNK)
        def _(d):
            outgoing_query(d).wait_recv()
            place_query(chip ^ d)

        base = (chip // CHUNK ^ part) * CHUNK

        @pl.loop(0, slots // 8 // UNROLL)
        def _(at_group):
            attend_groups(base, [at_group * UNROLL + u for u in range(UNROLL)])

        finish(max(first_d, 1), first_d + CHUNK)

    o_ref[chip] = answer(chip)
    own_forward().wait_send()

    @pl.loop(1, chips)
    def _(d):
        outgoing(d).wait_send()
        outgoing_query(d).wait_send()
        forward(d).wait_send()
        reply(d).wait()


def by_head(queries, key_rows, value_rows, key_scale, value_scale, cluster_label):
    tok, heads, width = queries.shape
    half = lax.axis_size("inner") // 2
    chips = lax.axis_size("outer") * half
    clusters = COARSE * FINE
    capacity = max(2, 2 * tok // clusters)
    slots = clusters * capacity
    labels = cluster_label[:, :, 0]
    earlier = jnp.arange(tok)[None, :] < jnp.arange(tok)[:, None]
    rank = jnp.sum(
        ((labels[:, :, None] == labels[:, None, :]) & earlier[None]).astype(jnp.int32), axis=2
    )
    aux = jnp.stack(
        [
            key_scale.T,
            value_scale.T,
            (labels * capacity).astype(jnp.bfloat16),
            rank.astype(jnp.bfloat16),
        ],
        axis=1,
    )
    aux = jnp.pad(aux, ((0, 0), (0, AUX - 4), (0, 0)))
    aux = aux.reshape(heads, AUX, tok // width, width).swapaxes(1, 2).reshape(heads, -1, width)
    packed = jnp.concatenate(
        [
            key_rows.swapaxes(0, 1),
            value_rows.swapaxes(0, 1),
            aux,
            queries.swapaxes(0, 1),
        ],
        axis=1,
    )
    vm = pl.BlockSpec(memory_space=pltpu.VMEM)
    dma = pltpu.SemaphoreType.DMA
    f32 = jnp.float32
    returned = pl.pallas_call(
        lambda *refs: exchange_kernel(chips, half, tok, slots, *refs),
        out_shape=jax.ShapeDtypeStruct((heads, tok, width), jnp.bfloat16),
        in_specs=[vm],
        out_specs=vm,
        scratch_shapes=[
            pltpu.VMEM((2 * chips,) + packed.shape[1:], jnp.bfloat16),
            pltpu.VMEM((chips, tok, width), jnp.bfloat16),
            pltpu.VMEM((2 * chips, slots, width), f32),
            pltpu.VMEM((2 * chips, slots, width), f32),
            pltpu.VMEM((2 * chips, slots, width), f32),
            pltpu.VMEM((chips, slots, width), f32),
            pltpu.VMEM((chips, slots, width), f32),
            pltpu.VMEM((slots // 8, 16 * chips, width), jnp.bfloat16),
            pltpu.VMEM((slots // 8, 16 * chips, width), jnp.bfloat16),
            pltpu.VMEM((slots // 8, 16, 16 * chips), f32),
            pltpu.VMEM((8 * chips, 16 * chips), f32),
        ]
        + [dma((chips,))] * 8,
        compiler_params=pltpu.CompilerParams(
            collective_id=0, has_side_effects=True, vmem_limit_bytes=62 * 1024 * 1024
        ),
        name="clustered",
    )(packed)
    return returned.swapaxes(0, 1)


UNROLL = 16
CHUNK = 4


def route(queries, key_rows, value_rows, key_scale, value_scale, cluster_label):
    tok, heads, width = queries.shape
    devices = lax.axis_size("outer") * lax.axis_size("inner")
    even = lax.axis_size("inner") % 2 == 0 and tok == 2 * width
    even = even and heads & (heads - 1) == 0 and heads % CHUNK == 0
    if devices == 2 * heads and even and 2 * tok == 4 * COARSE * FINE:
        return by_head(queries, key_rows, value_rows, key_scale, value_scale, cluster_label)
    return shards(queries, key_rows, value_rows, key_scale, value_scale, cluster_label)


def solution(mesh):
    placed = (
        P(("outer", "inner"), None, None),
        P(("outer", "inner"), None, None),
        P(("outer", "inner"), None, None),
        P(("outer", "inner"), None),
        P(("outer", "inner"), None),
        P(None, ("outer", "inner"), None),
    )
    return jax.shard_map(
        route,
        mesh=mesh,
        in_specs=placed,
        out_specs=P(("outer", "inner"), None, None),
        check_vma=False,
    )
```

profile of v0, /device:TPU:0, one launch (start us, length us, event | category | flops | bytes accessed | tf_op | source)
XLA Modules:
  0.0 115.6 jit_solution(14027694903336505980)
XLA Ops:
  0.0 0.0 copy-start.1
  0.0 0.0 copy-start
  0.0 0.9 fusion.7
  0.9 1.3 %convert_reduce_fusion = s32[16,256]{1,0:T(8,128)S(1)} fusion(s32[16,256]{1,0:T(8,128)S(1)} %get-tuple-element.6, pred[256,256]{1,0:T(8,128)(4,1)S(1)} %iota_compare_fusion), kind=kLoop, calls=%fused_computation | loop fusion | flops 4190208 | bytes 98304 | tf_op jit(solution)/shard_map/reduce_sum | solution.py:406
  2.2 0.7 fusion.6
  3.0 1.5 %copy.27 = bf16[256,16,128]{2,0,1:T(8,128)(2,1)S(1)} copy(bf16[256,16,128]{2,1,0:T(8,128)(2,1)} %param.7) | data formatting | bytes 2097152 | tf_op args[1]
  4.5 0.0 copy-done.1
  4.5 0.0 copy-done
  4.5 0.5 copy_bitcast_fusion
  5.1 1.8 %pad_maximum_fusion.refs_0_ = bf16[16,784,128]{2,1,0:T(8,128)(2,1)} fusion(bf16[16,256,128]{2,1,0:T(8,128)(2,1)S(1)} %get-tuple-element.7, bf16[16,16,128]{2,1,0:T(8,128)(2,1)S(1)} %bitcast.29, bf16[16,256,128]{2,1,0:T(8,128)(2,1)S(1)} %get-tuple-element.8, bf16[16,256,128]{2,1,0:T(8,128)(2,1)S(1)} %bitcast.27), kind=kLoop, calls=%fused_computation.1 | loop fusion | flops 12845056 | bytes 6422528 | tf_op jit(solution)/shard_map/concatenate | solution.py:420
  6.9 105.8 %clustered.1 = bf16[16,256,128]{2,1,0:T(8,128)(2,1)} custom-call(bf16[16,784,128]{2,1,0:T(8,128)(2,1)} %pad_maximum_fusion.refs_0_), custom_call_target="tpu_custom_call" | custom-call | tf_op jit(solution)/shard_map/clustered/pallas_call | solution.py:432
  112.7 2.9 %copy.17 = bf16[256,16,128]{2,1,0:T(8,128)(2,1)} copy(bf16[256,16,128]{2,0,1:T(8,128)(2,1)} %bitcast.28) | data formatting | bytes 2097152 | tf_op jit(solution)/shard_map/transpose | solution.py:456
  (4 shorter events, 0.1 us)
Async XLA Ops:
  0.0 4.5 %copy-start.1 = (bf16[256,16,128]{2,1,0:T(8,128)(2,1)S(1)}, bf16[256,16,128]{2,1,0:T(8,128)(2,1)}, u32[]{:S(2)}) copy-start(bf16[256,16,128]{2,1,0:T(8,128)(2,1)} %param.8) | copy-start | bytes 3145732
  0.0 4.5 %copy-start = (bf16[256,16,128]{2,1,0:T(8,128)(2,1)S(1)}, bf16[256,16,128]{2,1,0:T(8,128)(2,1)}, u32[]{:S(2)}) copy-start(bf16[256,16,128]{2,1,0:T(8,128)(2,1)} %param.6) | copy-start | bytes 3145732
where the time goes:
time: 116 us
  Pallas kernels  106 us (91%)
  local copies, waits for them, and re-layouts  4.97 us (4%)
  other arithmetic  4.73 us (4%)
    pallas_call x1, Pallas kernels, by_head(): pl.pallas_call(lambda *refs: exchange_kernel(chips, half, tok, slots, *re...  106 us
    transpose x1, local copies, waits for them, and re-layouts, by_head(): return returned.swapaxes(0, 1)  2.87 us

commit v1 on v0

--- a/solution.py
+++ b/solution.py
@@ -144,21 +144,25 @@
     rows_back = returned.reshape(total, width)
     return rows_back[flat].reshape(tok_rows, heads, width)
 
-AUX = 8
+AUX = 4
 
 
 def exchange_kernel(
-    chips, half, tok, slots, x_ref, o_ref, recv, ans, kp, vp, xp, qp, op, kb, vb, scales, vis_ref,
-    send_sem, recv_sem, fsend, frecv, qsend, qrecv, bsend, brecv,
+    chips, half, tok, slots, k_in, v_in, q_in, ks_ref, vs_ref, label_ref, out_ref,
+    raw, kv, qt, aux, recv, recv_q, recv_aux, ans, back, kp, vp, xp, qp, op, kb, vb, scales,
+    vis_ref, f_scale, load_sem, asend, arecv, send_sem, recv_sem, fasend, farecv, fsend, frecv,
+    qsend, qrecv, bsend, brecv,
 ):
     f32, bf16 = jnp.float32, jnp.bfloat16
-    width = x_ref.shape[2]
+    width = kv.shape[2]
     inner = lax.axis_index("inner")
     chip = lax.axis_index("outer") * half + inner // 2
     core = inner % 2
+    mine = 2 * chip + core
     partner = {"outer": lax.axis_index("outer"), "inner": inner + 1 - 2 * core}
-    first = x_ref.shape[1] - tok
-    first_rows, query_rows = pl.ds(0, first), pl.ds(first, tok)
+    far_bit = half // 2
+    crossing = [d for d in range(1, chips) if d & far_bit]
+    staying = [d for d in range(1, chips) if not d & far_bit]
 
     def at(other):
         return {"outer": other // half, "inner": (other % half) * 2 + core}
@@ -181,107 +185,160 @@
     pl.semaphore_signal(
         barrier, inc=1, device_id=partner, device_id_type=pl.DeviceIdType.MESH
     )
+
+    def load(which, source):
+        return pltpu.make_async_copy(source, raw.at[which], load_sem.at[which])
+
+    load(0, k_in).start()
+    load(1, v_in).start()
+    load(2, q_in).start()
+
+    clusters = COARSE * FINE
+    capacity = slots // clusters
+    earlier = (
+        lax.broadcasted_iota(jnp.int32, (tok, tok), 0)
+        < lax.broadcasted_iota(jnp.int32, (tok, tok), 1)
+    ).astype(f32).astype(bf16)
+    f_scale[0] = ks_ref[...].astype(f32)
+    f_scale[1] = vs_ref[...].astype(f32)
+    aux_row = lax.broadcasted_iota(jnp.int32, (AUX, tok), 0)
+
+    @pl.loop(0, chips)
+    def _(h):
+        label = label_ref[h]
+        member = jnp.where(
+            lax.broadcasted_iota(jnp.int32, (clusters, tok), 0) == label, f32(1.0), f32(0.0)
+        )
+        before = jnp.dot(member.astype(bf16), earlier, preferred_element_type=f32)
+        rank = jnp.sum(before * member, axis=0, keepdims=True)
+        first_two = jnp.where(
+            aux_row == 0, f_scale[0, pl.ds(h, 1), :], f_scale[1, pl.ds(h, 1), :]
+        )
+        last_two = jnp.where(aux_row == 2, (label * capacity).astype(f32), rank)
+        aux[h] = jnp.where(aux_row < 2, first_two, last_two).astype(bf16)
+
+    load(0, k_in).wait()
+    kv[:, :tok, :] = jnp.swapaxes(raw[0], 0, 1)
+    load(1, v_in).wait()
+    kv[:, tok:, :] = jnp.swapaxes(raw[1], 0, 1)
     pl.semaphore_wait(barrier, chips)
+
+    def out_aux(d):
+        other = chip ^ d
+        return copy(aux.at[other], recv_aux.at[mine], asend.at[d], arecv.at[d], at(other))
 
     def outgoing(d):
         other = chip ^ d
-        return copy(
-            x_ref.at[other, first_rows], recv.at[2 * chip + core, first_rows],
-            send_sem.at[d], recv_sem.at[d], at(other),
-        )
+        return copy(kv.at[other], recv.at[mine], send_sem.at[d], recv_sem.at[d], at(other))
 
     def outgoing_query(d):
         other = chip ^ d
-        return copy(
-            x_ref.at[other, query_rows], recv.at[2 * chip + core, query_rows],
-            qsend.at[d], qrecv.at[d], at(other),
-        )
-
-    @pl.loop(1, chips)
-    def _(d):
-        outgoing(d).start()
-
-    @pl.loop(1, chips)
-    def _(d):
-        outgoing_query(d).start()
+        return copy(qt.at[other], recv_q.at[chip], qsend.at[d], qrecv.at[d], at(other))
+
+    def own_aux():
+        return copy(aux.at[chip], recv_aux.at[mine], fasend.at[0], farecv.at[0], partner)
 
     def own_forward():
-        return copy(
-            x_ref.at[chip, first_rows], recv.at[2 * chip + core, first_rows],
-            fsend.at[0], frecv.at[0], partner,
-        )
+        return copy(kv.at[chip], recv.at[mine], fsend.at[0], frecv.at[0], partner)
+
+    def forward_aux(d):
+        row = 2 * (chip ^ d) + core
+        return copy(recv_aux.at[row], recv_aux.at[row], fasend.at[d], farecv.at[d], partner)
 
     def forward(d):
         row = 2 * (chip ^ d) + core
-        return copy(
-            recv.at[row, first_rows], recv.at[row, first_rows], fsend.at[d], frecv.at[d], partner
-        )
-
+        return copy(recv.at[row], recv.at[row], fsend.at[d], frecv.at[d], partner)
+
+    for d in crossing + staying:
+        out_aux(d).start()
+    own_aux().start()
+    for i, d in enumerate(crossing):
+        outgoing(d).start()
+        if i < len(staying):
+            outgoing(staying[i]).start()
     own_forward().start()
-    recv[2 * chip + core] = x_ref[chip]
+    load(2, q_in).wait()
+    qt[...] = jnp.swapaxes(raw[2], 0, 1)
 
     lane = lax.broadcasted_iota(jnp.int32, (tok, width), 1)
     low = (lane < width // 2).astype(f32).astype(bf16)
     high = (lane >= width // 2).astype(f32).astype(bf16)
+
+    for d in staying + crossing:
+        outgoing_query(d).start()
+
+    recv[mine] = kv[chip]
+    recv_aux[mine] = aux[chip]
+    recv_q[chip] = qt[chip]
+
     key_at = lax.broadcasted_iota(jnp.int32, vis_ref.shape, 1)
     query_at = lax.broadcasted_iota(jnp.int32, vis_ref.shape, 0)
+    turn = query_at // 8
+    away = turn % far_bit + (turn // far_bit) % (chips // 2 // far_bit) * (2 * far_bit)
+    away = away + turn // (chips // 2) * far_bit
     key_order = (key_at // 8) * 4 + key_at % 4
-    query_order = (2 * (query_at // 8) + core) * 4 + query_at % 4
+    query_order = (2 * (away ^ chip) + core) * 4 + query_at % 4
     same = (key_at // 4) % 2 == (query_at // 4) % 2
     vis_ref[...] = jnp.where(same & (key_order <= query_order), f32(1.0), f32(0.0))
-    halves = tok // width
+    turns = [0] + staying + crossing
 
     def aux_of(row):
-        block = recv[row, pl.ds(2 * tok, AUX * halves)].astype(f32)
-        return jnp.concatenate(
-            [block[AUX * i : AUX * (i + 1)] for i in range(halves)], axis=1
-        )
-
-    def hits(aux):
-        slot = (aux[2:3] + aux[3:4]).astype(jnp.int32)
+        return recv_aux[row].astype(f32)
+
+    def hits(extra):
+        slot = (extra[2:3] + extra[3:4]).astype(jnp.int32)
         return lax.broadcasted_iota(jnp.int32, (slots, tok), 0) == slot
 
     def one_hot(hit):
         return jnp.where(hit, f32(1.0), f32(0.0)).astype(bf16)
 
     def place(row):
-        aux = aux_of(row)
-        hit = hits(aux)
+        extra = aux_of(row)
+        hit = hits(extra)
         one = one_hot(hit)
-        by_key = jnp.where(hit, aux[0:1], f32(0.0)).astype(bf16)
-        by_value = jnp.where(hit, aux[1:2], f32(0.0)).astype(bf16)
+        by_key = jnp.where(hit, extra[0:1], f32(0.0)).astype(bf16)
+        by_value = jnp.where(hit, extra[1:2], f32(0.0)).astype(bf16)
         kp[row] = jnp.dot(one, recv[row, pl.ds(0, tok)], preferred_element_type=f32)
         vp[row] = jnp.dot(one, recv[row, pl.ds(tok, tok)], preferred_element_type=f32)
         xp[row] = jnp.dot(by_key, low, preferred_element_type=f32) + jnp.dot(
             by_value, high, preferred_element_type=f32
         )
 
-    def place_query(other):
-        row = 2 * other + core
-        qp[other] = jnp.dot(
-            one_hot(hits(aux_of(row))), recv[row, query_rows], preferred_element_type=f32
-        )
-
-    place(2 * chip + core)
+    def place_query(turn, other):
+        qp[turn] = jnp.dot(
+            one_hot(hits(aux_of(2 * other + core))), recv_q[other], preferred_element_type=f32
+        )
+
+    place(mine)
+    own_aux().wait_recv()
+    own_forward().wait_recv()
+    place(2 * chip + 1 - core)
+
+    def of_turn(t):
+        side = chips // 2
+        low_part = t % far_bit + (t // far_bit) % (side // far_bit) * (2 * far_bit)
+        return low_part + t // side * far_bit
 
     @pl.loop(1, chips)
-    def _(d):
+    def _(t):
+        d = of_turn(t)
+        out_aux(d).wait_recv()
+        forward_aux(d).start()
         outgoing(d).wait_recv()
         forward(d).start()
         place(2 * (chip ^ d) + core)
 
-        @pl.when(d == 1)
+        @pl.when(t > 1)
         def _():
-            own_forward().wait_recv()
-
-        @pl.when(d > 1)
-        def _():
-            forward(d - 1).wait_recv()
-
-        place(2 * (chip ^ (d - 1)) + 1 - core)
-
-    forward(chips - 1).wait_recv()
-    place(2 * (chip ^ (chips - 1)) + 1 - core)
+            before = of_turn(t - 1)
+            forward_aux(before).wait_recv()
+            forward(before).wait_recv()
+            place(2 * (chip ^ before) + 1 - core)
+
+    last = turns[-1]
+    forward_aux(last).wait_recv()
+    forward(last).wait_recv()
+    place(2 * (chip ^ last) + 1 - core)
 
     sel_lane = lax.broadcasted_iota(jnp.int32, (16, width), 1)
     sel_row = lax.broadcasted_iota(jnp.int32, (16, width), 0)
@@ -306,7 +363,7 @@
 
     def attend_groups(base, groups):
         here = pl.ds(base, CHUNK)
-        allowed = vis_ref[pl.ds(pl.multiple_of(base * 8, chunk_rows), chunk_rows), :]
+        allowed = vis_ref[pl.ds(base * 8, chunk_rows), :]
         scale = [scales[t] for t in groups]
         query = [qp[here, rows_of(t), :].reshape(chunk_rows, width).astype(bf16) for t in groups]
         scores = [
@@ -338,60 +395,60 @@
         == lax.broadcasted_iota(jnp.int32, (tok, tok), 1)
     ).astype(f32).astype(bf16)
 
-    def answer(other):
+    def answer(turn, other):
         columns = lax.dot_general(
-            eye,
-            aux_of(2 * other + core).astype(bf16),
-            (((1,), (1,)), ((), ())),
-            preferred_element_type=f32,
+            eye, recv_aux[2 * other + core], (((1,), (1,)), ((), ())), preferred_element_type=f32,
         )
         slot = (columns[:, 2:3] + columns[:, 3:4]).astype(jnp.int32)
         hit = lax.broadcasted_iota(jnp.int32, (tok, slots), 1) == slot
-        one = jnp.where(hit, f32(1.0), f32(0.0)).astype(bf16)
-        return jnp.dot(one, op[other].astype(bf16), preferred_element_type=f32).astype(bf16)
+        return jnp.dot(
+            one_hot(hit), op[turn].astype(bf16), preferred_element_type=f32
+        ).astype(bf16)
 
     def reply(d):
         other = chip ^ d
-        return copy(ans.at[other], o_ref.at[chip], bsend.at[d], brecv.at[d], at(other))
-
-    def finish(first_d, last_d):
-        @pl.loop(first_d, last_d)
-        def _(d):
-            other = chip ^ d
-            ans[other] = answer(other)
-
-            @pl.when(d > first_d)
-            def _():
-                reply(d - 1).start()
-
-        reply(last_d - 1).start()
-
-    place_query(chip)
+        return copy(ans.at[other], back.at[chip], bsend.at[d], brecv.at[d], at(other))
+
+    place_query(0, chip)
     for part in range(chips // CHUNK):
-        first_d = part * CHUNK
-
-        @pl.loop(max(first_d, 1), first_d + CHUNK)
-        def _(d):
+        first_turn = part * CHUNK
+        start = max(first_turn, 1)
+
+        @pl.loop(start, first_turn + CHUNK)
+        def _(t):
+            d = of_turn(t)
             outgoing_query(d).wait_recv()
-            place_query(chip ^ d)
-
-        base = (chip // CHUNK ^ part) * CHUNK
+            place_query(t, chip ^ d)
 
         @pl.loop(0, slots // 8 // UNROLL)
         def _(at_group):
-            attend_groups(base, [at_group * UNROLL + u for u in range(UNROLL)])
-
-        finish(max(first_d, 1), first_d + CHUNK)
-
-    o_ref[chip] = answer(chip)
+            attend_groups(first_turn, [at_group * UNROLL + u for u in range(UNROLL)])
+
+        @pl.loop(start, first_turn + CHUNK)
+        def _(t):
+            other = chip ^ of_turn(t)
+            ans[other] = answer(t, other)
+
+            @pl.when(t > start)
+            def _():
+                reply(of_turn(t - 1)).start()
+
+        reply(of_turn(first_turn + CHUNK - 1)).start()
+
+    back[chip] = answer(0, chip)
     own_forward().wait_send()
+    own_aux().wait_send()
 
     @pl.loop(1, chips)
     def _(d):
+        out_aux(d).wait_send()
         outgoing(d).wait_send()
         outgoing_query(d).wait_send()
+        forward_aux(d).wait_send()
         forward(d).wait_send()
         reply(d).wait()
+
+    out_ref[...] = jnp.swapaxes(back[...], 0, 1)
 
 
 def by_head(queries, key_rows, value_rows, key_scale, value_scale, cluster_label):
@@ -399,61 +456,46 @@
     half = lax.axis_size("inner") // 2
     chips = lax.axis_size("outer") * half
     clusters = COARSE * FINE
-    capacity = max(2, 2 * tok // clusters)
-    slots = clusters * capacity
-    labels = cluster_label[:, :, 0]
-    earlier = jnp.arange(tok)[None, :] < jnp.arange(tok)[:, None]
-    rank = jnp.sum(
-        ((labels[:, :, None] == labels[:, None, :]) & earlier[None]).astype(jnp.int32), axis=2
-    )
-    aux = jnp.stack(
-        [
-            key_scale.T,
-            value_scale.T,
-            (labels * capacity).astype(jnp.bfloat16),
-            rank.astype(jnp.bfloat16),
-        ],
-        axis=1,
-    )
-    aux = jnp.pad(aux, ((0, 0), (0, AUX - 4), (0, 0)))
-    aux = aux.reshape(heads, AUX, tok // width, width).swapaxes(1, 2).reshape(heads, -1, width)
-    packed = jnp.concatenate(
-        [
-            key_rows.swapaxes(0, 1),
-            value_rows.swapaxes(0, 1),
-            aux,
-            queries.swapaxes(0, 1),
-        ],
-        axis=1,
-    )
+    slots = clusters * max(2, 2 * tok // clusters)
     vm = pl.BlockSpec(memory_space=pltpu.VMEM)
+    anywhere = pl.BlockSpec(memory_space=pl.ANY)
     dma = pltpu.SemaphoreType.DMA
-    f32 = jnp.float32
-    returned = pl.pallas_call(
+    f32, bf16 = jnp.float32, jnp.bfloat16
+    return pl.pallas_call(
         lambda *refs: exchange_kernel(chips, half, tok, slots, *refs),
-        out_shape=jax.ShapeDtypeStruct((heads, tok, width), jnp.bfloat16),
-        in_specs=[vm],
+        out_shape=jax.ShapeDtypeStruct((tok, heads, width), bf16),
+        in_specs=[anywhere] * 3 + [vm] * 3,
         out_specs=vm,
         scratch_shapes=[
-            pltpu.VMEM((2 * chips,) + packed.shape[1:], jnp.bfloat16),
-            pltpu.VMEM((chips, tok, width), jnp.bfloat16),
+            pltpu.VMEM((3, tok, heads, width), bf16),
+            pltpu.VMEM((heads, 2 * tok, width), bf16),
+            pltpu.VMEM((heads, tok, width), bf16),
+            pltpu.VMEM((heads, AUX, tok), bf16),
+            pltpu.VMEM((2 * chips, 2 * tok, width), bf16),
+            pltpu.VMEM((chips, tok, width), bf16),
+            pltpu.VMEM((2 * chips, AUX, tok), bf16),
+            pltpu.VMEM((chips, tok, width), bf16),
+            pltpu.VMEM((chips, tok, width), bf16),
             pltpu.VMEM((2 * chips, slots, width), f32),
             pltpu.VMEM((2 * chips, slots, width), f32),
             pltpu.VMEM((2 * chips, slots, width), f32),
             pltpu.VMEM((chips, slots, width), f32),
             pltpu.VMEM((chips, slots, width), f32),
-            pltpu.VMEM((slots // 8, 16 * chips, width), jnp.bfloat16),
-            pltpu.VMEM((slots // 8, 16 * chips, width), jnp.bfloat16),
+            pltpu.VMEM((slots // 8, 16 * chips, width), bf16),
+            pltpu.VMEM((slots // 8, 16 * chips, width), bf16),
             pltpu.VMEM((slots // 8, 16, 16 * chips), f32),
             pltpu.VMEM((8 * chips, 16 * chips), f32),
+            pltpu.VMEM((2, heads, tok), f32),
+            dma((3,)),
         ]
-        + [dma((chips,))] * 8,
+        + [dma((chips,))] * 12,
         compiler_params=pltpu.CompilerParams(
-            collective_id=0, has_side_effects=True, vmem_limit_bytes=62 * 1024 * 1024
+            collective_id=0, has_side_effects=True, vmem_limit_bytes=63 * 1024 * 1024
         ),
         name="clustered",
-    )(packed)
-    return returned.swapaxes(0, 1)
+    )(
+        key_rows, value_rows, queries, key_scale.T, value_scale.T, cluster_label.swapaxes(1, 2)
+    )
 
 
 UNROLL = 16

time: 116 us -> 117 us (level)
  Pallas kernels: 106 us -> 115 us
  other arithmetic: 4.73 us -> 0 us
  local copies, waits for them, and re-layouts: 4.97 us -> 2.37 us
    pallas_call x1, Pallas kernels: 106 us -> 115 us  [by_head(): pl.pallas_call(lambda *refs: exchange_kernel(chips, half, tok, slots, *re...]
    transpose x2 -> x0, local copies, waits for them, and re-layouts: 3.42 us -> none  [the longest x1 2.87 us: by_head(): return returned.swapaxes(0, 1)]
    concatenate x1 -> x0, other arithmetic: 1.8 us -> none  [by_head(): jnp.concatenate([key_rows.swapaxes(0, 1), value_rows.swapaxes(0, 1), aux,...]
    reduce_sum x1 -> x0, other arithmetic: 1.3 us -> none  [by_head(): jnp.sum(((labels[:, :, None] == labels[:, None, :]) & earlier[None]).asty...]
    unnamed x5 -> x1, local copies, waits for them, and re-layouts: 1.51 us -> 2.37 us
where the time goes in v1:
time: 117 us
  Pallas kernels  115 us (98%)
  local copies, waits for them, and re-layouts  2.37 us (2%)
    pallas_call x1, Pallas kernels, by_head(): pl.pallas_call(lambda *refs: exchange_kernel(chips, half, tok, slots, *re...  115 us
    unnamed x1, local copies, waits for them, and re-layouts  2.37 us

profile of v1, /device:TPU:0, one launch (start us, length us, event | category | flops | bytes accessed | tf_op | source)
XLA Modules:
  0.0 116.9 jit_solution(14595720471634459732)
XLA Ops:
  0.0 114.6 %clustered.1 = bf16[256,16,128]{2,1,0:T(8,128)(2,1)} custom-call(bf16[256,16,128]{2,1,0:T(8,128)(2,1)} %refs_0_.1, bf16[256,16,128]{2,1,0:T(8,128)(2,1)} %refs_1_.1, bf16[256,16,128]{2,1,0:T(8,128)(2,1)} %refs_2_.1, bf16[16,256]{1,0:T(8,128)(2,1)} %bitcast.4, bf16[16,256]{1,0:T(8,128)(2,1)} %bitcast.5, s32[16,1,256]{2,1,0:T(1,128)} %bitcast.3), custom_call_target="tpu_custom_call" | custom-call | tf_op jit(solution)/shard_map/clustered/pallas_call | solution.py:464
  114.6 2.4 %copy.8 = bf16[256,16,128]{2,1,0:T(8,128)(2,1)} copy(bf16[256,16,128]{2,1,0:T(8,128)(2,1)} %clustered.1) | data formatting | bytes 2097152

commit v2 on v1

--- a/solution.py
+++ b/solution.py
@@ -252,10 +252,8 @@
     for d in crossing + staying:
         out_aux(d).start()
     own_aux().start()
-    for i, d in enumerate(crossing):
+    for d in range(1, chips):
         outgoing(d).start()
-        if i < len(staying):
-            outgoing(staying[i]).start()
     own_forward().start()
     load(2, q_in).wait()
     qt[...] = jnp.swapaxes(raw[2], 0, 1)
@@ -264,7 +262,7 @@
     low = (lane < width // 2).astype(f32).astype(bf16)
     high = (lane >= width // 2).astype(f32).astype(bf16)
 
-    for d in staying + crossing:
+    for d in range(1, chips):
         outgoing_query(d).start()
 
     recv[mine] = kv[chip]
@@ -274,13 +272,12 @@
     key_at = lax.broadcasted_iota(jnp.int32, vis_ref.shape, 1)
     query_at = lax.broadcasted_iota(jnp.int32, vis_ref.shape, 0)
     turn = query_at // 8
-    away = turn % far_bit + (turn // far_bit) % (chips // 2 // far_bit) * (2 * far_bit)
-    away = away + turn // (chips // 2) * far_bit
+    away = turn
     key_order = (key_at // 8) * 4 + key_at % 4
     query_order = (2 * (away ^ chip) + core) * 4 + query_at % 4
     same = (key_at // 4) % 2 == (query_at // 4) % 2
     vis_ref[...] = jnp.where(same & (key_order <= query_order), f32(1.0), f32(0.0))
-    turns = [0] + staying + crossing
+    turns = list(range(chips))
 
     def aux_of(row):
         return recv_aux[row].astype(f32)
@@ -315,9 +312,7 @@
     place(2 * chip + 1 - core)
 
     def of_turn(t):
-        side = chips // 2
-        low_part = t % far_bit + (t // far_bit) % (side // far_bit) * (2 * far_bit)
-        return low_part + t // side * far_bit
+        return t
 
     @pl.loop(1, chips)
     def _(t):

time: 117 us -> 108 us (0.923)
  Pallas kernels: 115 us -> 106 us
    pallas_call x1, Pallas kernels: 115 us -> 106 us  [by_head(): pl.pallas_call(lambda *refs: exchange_kernel(chips, half, tok, slots, *re...]
where the time goes in v2:
time: 108 us
  Pallas kernels  106 us (98%)
  local copies, waits for them, and re-layouts  2.37 us (2%)
    pallas_call x1, Pallas kernels, by_head(): pl.pallas_call(lambda *refs: exchange_kernel(chips, half, tok, slots, *re...  106 us
    unnamed x1, local copies, waits for them, and re-layouts  2.37 us

profile of v2, /device:TPU:0, one launch (start us, length us, event | category | flops | bytes accessed | tf_op | source)
XLA Modules:
  0.0 108.1 jit_solution(16383504851708270097)
XLA Ops:
  0.0 105.7 %clustered.1 = bf16[256,16,128]{2,1,0:T(8,128)(2,1)} custom-call(bf16[256,16,128]{2,1,0:T(8,128)(2,1)} %refs_0_.1, bf16[256,16,128]{2,1,0:T(8,128)(2,1)} %refs_1_.1, bf16[256,16,128]{2,1,0:T(8,128)(2,1)} %refs_2_.1, bf16[16,256]{1,0:T(8,128)(2,1)} %bitcast.4, bf16[16,256]{1,0:T(8,128)(2,1)} %bitcast.5, s32[16,1,256]{2,1,0:T(1,128)} %bitcast.3), custom_call_target="tpu_custom_call" | custom-call | tf_op jit(solution)/shard_map/clustered/pallas_call | solution.py:459
  105.7 2.4 %copy.8 = bf16[256,16,128]{2,1,0:T(8,128)(2,1)} copy(bf16[256,16,128]{2,1,0:T(8,128)(2,1)} %clustered.1) | data formatting | bytes 2097152
